TPU v7x, 32 devices: a whole 2x2x4 slice. The times are simulated.
32 devices in a mesh: grp: 2 (over x), seq: 16 (over z, y, core).
Axes of the slice: x: 2, y: 2, z: 4, core: 2. Of those that a mesh axis runs over, the one named last changes fastest.
Arguments:
- queries: bfloat16 [8, 4096], P('grp', 'seq'), parts along dimension 0, may hold values from -40 to 40
- gate_logits: float32 [8, 64], P('grp'), parts along dimension 0, may hold values from -6 to 6
- kv_pool: bfloat16 [512, 128, 2048], P(('grp', 'seq')), parts along dimension 0, may hold values from -6 to 6
- page_table: int32 [8, 64], P('grp'), parts along dimension 0, may hold values from 0 to 255, as said below
- selected: int32 [8, 8, 16], P('grp'), parts along dimension 0, may hold values from 0 to 63, as said below
- lengths: int32 [8], P('grp'), parts along dimension 0, may hold values from 4096 to 8192, as said below
Outputs:
- attended: bfloat16 [8, 4096], P('grp', 'seq'), parts along dimension 0
There are 2 independent parts, one for each index of `grp`. A program takes and returns all parts, laid end to end along the dimension named above; each array names one. Nothing has to cross between parts.
Inputs may be any that keep to these rules, and one draw needn't show every extreme that they name: `page_table`: a one-to-one map of the 4 x 64 pages onto the pool slots; each aligned run of 2 pages of a request lies in 2 consecutive slots starting at a multiple of 2. `lengths`: some request in every draw has length 8192. `selected`: for each request and key-value head, 16 different pages, all among the request's last 32 live pages, the last live page among them.
All inputs are finite; a program needn't handle non-finite values.
Results may differ from a plain program's by a relative error of at most 0.0039.
Values may be sent and summed in bfloat16 or wider, within the bound.
A program may use at most 64 MiB of HBM per device.

v0:
```python
import math
import jax
import jax.numpy as jnp
from jax import lax
from jax.sharding import PartitionSpec as P

HEAD_DIM = 128
neg_big = -1e30


def joined(part, axis, combine):
    gathered = jax.tree.map(lambda a: lax.all_gather(a, axis), part)

    def take(source):
        return jax.tree.map(lambda a: lax.dynamic_index_in_dim(a, source, 0, False), gathered)

    return lax.fori_loop(
        1, lax.axis_size(axis), lambda source, state: combine(state, take(source)), take(0)
    )


def merge_pair(left, right):
    merged = ()
    for offset in (0, 3):
        row_top = jnp.maximum(left[offset], right[offset])
        left_scale = jnp.exp(left[offset] - row_top)
        right_scale = jnp.exp(right[offset] - row_top)
        merged = merged + (
            row_top,
            left[offset + 1] * left_scale + right[offset + 1] * right_scale,
            left[offset + 2] * left_scale[..., None] + right[offset + 2] * right_scale[..., None],
        )
    return merged


def per_device(queries, gate_logits, kv_pool, page_table, selected, lengths):
    slot_count, page_len, double_width = kv_pool.shape
    kv_width = double_width // 2
    kv_heads = kv_width // HEAD_DIM
    requests = page_table.shape[0]
    ctx_pages = page_table.shape[1]
    col_count = queries.shape[1]
    highest = lax.Precision.HIGHEST
    all_queries = lax.all_gather(queries, "seq", axis=1, tiled=True)
    head_count = all_queries.shape[1] // HEAD_DIM
    group_size = head_count // kv_heads
    score_scale = 1.0 / math.sqrt(HEAD_DIM)
    first_slot = lax.axis_index("seq") * slot_count
    slot_ids = first_slot + jnp.arange(slot_count, dtype=jnp.int32)
    slot_match = page_table[:, :, None] == slot_ids[None, None, :]
    owner_hot = jnp.any(slot_match, axis=1)
    page_index = jnp.arange(ctx_pages, dtype=jnp.int32)
    page_of = jnp.sum(jnp.where(slot_match, page_index[None, :, None], 0), axis=(0, 1))
    slot_len = jnp.sum(jnp.where(owner_hot, lengths[:, None], 0), axis=0)
    owner_rows = jnp.dot(
        owner_hot.T.astype(jnp.bfloat16), all_queries, preferred_element_type=jnp.float32
    ).astype(jnp.bfloat16)
    slot_queries = owner_rows.reshape(slot_count, kv_heads, group_size, HEAD_DIM)
    key_rows = kv_pool[:, :, :kv_width].reshape(slot_count, page_len, kv_heads, HEAD_DIM)
    value_rows = kv_pool[:, :, kv_width:].reshape(slot_count, page_len, kv_heads, HEAD_DIM)
    position = page_of[:, None] * page_len + jnp.arange(page_len, dtype=jnp.int32)[None, :]
    is_valid = position < slot_len[:, None]
    is_live = page_of * page_len < slot_len
    valid_bf = is_valid.astype(jnp.bfloat16)
    counts = jnp.maximum(jnp.sum(is_valid.astype(jnp.float32), axis=1), 1.0)
    summary_keys = (
        jnp.einsum("st,stkd->skd", valid_bf, key_rows, preferred_element_type=jnp.float32)
        / counts[:, None, None]
    ).astype(jnp.bfloat16)
    summary_values = (
        jnp.einsum("st,stkd->skd", valid_bf, value_rows, preferred_element_type=jnp.float32)
        / counts[:, None, None]
    ).astype(jnp.bfloat16)
    coarse = (
        jnp.einsum("skgd,skd->skg", slot_queries, summary_keys, preferred_element_type=jnp.float32)
        * score_scale
    )
    coarse_mask = owner_hot[:, :, None, None] & is_live[None, :, None, None]
    coarse_masked = jnp.where(coarse_mask, coarse[None], neg_big)
    coarse_top = jnp.max(coarse_masked, axis=1)
    coarse_wt = jnp.where(coarse_mask, jnp.exp(coarse_masked - coarse_top[:, None]), 0.0)
    coarse_sum = jnp.sum(coarse_wt, axis=1)
    coarse_num = jnp.einsum(
        "rskg,skd->rkgd", coarse_wt, summary_values.astype(jnp.float32), precision=highest
    )
    fine_scores = (
        jnp.einsum("skgd,stkd->skgt", slot_queries, key_rows, preferred_element_type=jnp.float32)
        * score_scale
    )
    token_mask = is_valid[:, None, None, :]
    fine_masked = jnp.where(token_mask, fine_scores, neg_big)
    page_max = jnp.max(fine_masked, axis=3)
    page_wt = jnp.where(token_mask, jnp.exp(fine_masked - page_max[..., None]), 0.0).astype(
        jnp.bfloat16
    )
    page_sum = jnp.sum(page_wt.astype(jnp.float32), axis=3)
    page_num = jnp.einsum(
        "skgt,stkd->skgd", page_wt, value_rows, preferred_element_type=jnp.float32
    )
    page_hit = selected[:, None, :, :] == page_of[None, :, None, None]
    chosen = jnp.any(page_hit, axis=3) & owner_hot[:, :, None]
    chosen_full = chosen[..., None]
    sel_masked = jnp.where(chosen_full, page_max[None], neg_big)
    fine_top = jnp.max(sel_masked, axis=1)
    fine_wt = jnp.where(chosen_full, jnp.exp(sel_masked - fine_top[:, None]), 0.0)
    fine_sum = jnp.sum(fine_wt * page_sum[None], axis=1)
    fine_num = jnp.einsum("rskg,skgd->rkgd", fine_wt, page_num, precision=highest)
    gate_all = jax.nn.sigmoid(gate_logits)
    start_col = lax.axis_index("seq") * col_count
    coarse_gate = lax.dynamic_slice_in_dim(
        jnp.repeat(gate_all[:, :head_count], HEAD_DIM, axis=1), start_col, col_count, 1
    )
    fine_gate = lax.dynamic_slice_in_dim(
        jnp.repeat(gate_all[:, head_count:], HEAD_DIM, axis=1), start_col, col_count, 1
    )
    merged = joined(
        (coarse_top, coarse_sum, coarse_num, fine_top, fine_sum, fine_num), "seq", merge_pair
    )
    coarse_full = (merged[2] / merged[1][..., None]).reshape(requests, head_count * HEAD_DIM)
    fine_full = (merged[5] / merged[4][..., None]).reshape(requests, head_count * HEAD_DIM)
    coarse_cols = lax.dynamic_slice_in_dim(coarse_full, start_col, col_count, 1)
    fine_cols = lax.dynamic_slice_in_dim(fine_full, start_col, col_count, 1)
    return (coarse_gate * coarse_cols + fine_gate * fine_cols).astype(jnp.bfloat16)


def solution(mesh):
    return jax.shard_map(
        per_device,
        mesh=mesh,
        in_specs=(
            P("grp", "seq"),
            P("grp", None),
            P(("grp", "seq"), None, None),
            P("grp", None),
            P("grp", None, None),
            P("grp"),
        ),
        out_specs=P("grp", "seq"),
        check_vma=False,
    )
```

profile of v0, /device:TPU:0, one launch (start us, length us, event | category | flops | bytes accessed | tf_op | source)
XLA Modules:
  0.0 191.3 jit_solution(17139264196177832659)
XLA Ops:
  6.5 0.9 compare_reduce_fusion.1
  7.4 0.9 fusion.21
  8.3 0.7 select_reduce_fusion.2
  9.1 0.2 convert_reduce_fusion.1
  9.3 23.4 %all_gather.39 = bf16[4,4096]{1,0:T(4,128)(2,1)S(1)} all-gather(bf16[4,256]{1,0:T(4,128)(2,1)} %param.8), channel_id=1, replica_groups=mesh['grp'=2,'seq'=16] {'seq'}, dimensions={1}, use_global_device_ids=true | all-gather | bytes 34816 | tf_op jit(solution)/shard_map/all_gather | solution.py:44
  32.8 0.2 convolution_convert_fusion
  33.1 6.1 %fusion.43 = (bf16[16,128,1024]{2,1,0:T(8,128)(2,1)}, bf16[16,128,1024]{2,1,0:T(8,128)(2,1)}) fusion(bf16[16,128,2048]{2,1,0:T(8,128)(2,1)} %param.10), kind=kLoop, calls=%fused_computation.82 | loop fusion | bytes 16777216 | tf_op jit(solution)/shard_map/slice | solution.py:60
  39.2 6.4 %copy.115 = bf16[16,128,1024]{1,2,0:T(8,128)(2,1)} copy(bf16[16,128,1024]{2,1,0:T(8,128)(2,1)} %get-tuple-element.421) | data formatting | bytes 8388608
  45.6 6.4 %copy.114 = bf16[16,128,1024]{1,2,0:T(8,128)(2,1)} copy(bf16[16,128,1024]{2,1,0:T(8,128)(2,1)} %get-tuple-element.422) | data formatting | bytes 8388608
  52.0 3.5 %fusion.31 = f32[16,1,8,128]{3,1,2,0:T(1,128)S(1)} fusion(bf16[16,128,8,128]{1,3,2,0:T(8,128)(2,1)} %bitcast.92, pred[16,128,1,1]{1,0,2,3:T(8,128)(4,1)S(1)} %get-tuple-element.428), kind=kOutput, calls=%fused_computation.61 | convolution fusion | flops 4194304 | bytes 4261888 | tf_op jit(solution)/shard_map/st,stkd->skd/dot_general | solution.py:71
  55.5 1.2 fusion.33
  56.8 0.3 fusion.19
  57.1 0.1 copy.108
  57.3 0.2 fusion.11
  57.6 0.9 fusion.22
  58.5 1.2 compare_reduce_fusion
  59.9 3.5 %fusion.45 = (f32[16,8,4]{2,1,0:T(8,128)S(1)}, f32[16,8,4,128]{3,2,1,0:T(4,128)S(1)}) fusion(bf16[16,8,4,128]{3,2,1,0:T(4,128)(2,1)S(1)} %reshape.105, bf16[16,128,8,128]{1,3,2,0:T(8,128)(2,1)} %bitcast.94, pred[16,128]{1,0:T(8,128)(4,1)S(1)} %get-tuple-element.427), kind=kOutput, calls=%fused_computation.84 | convolution fusion | flops 16973312 | bytes 4591616 | tf_op jit(solution)/shard_map/skgd,stkd->skgt/dot_general | solution.py:87
  63.4 0.1 copy.92
  63.6 0.1 select_reduce_fusion
  63.7 4.5 %fusion.40 = f32[16,8,4,128]{3,2,1,0:T(4,128)S(1)} fusion(bf16[16,128,8,128]{1,3,2,0:T(8,128)(2,1)} %bitcast.93, f32[16,8,4,128]{3,2,1,0:T(4,128)S(1)} %get-tuple-element.430, f32[16,8,4]{2,1,0:T(8,128)S(1)} %get-tuple-element.429, pred[16,128]{1,0:T(8,128)(4,1)S(1)} %get-tuple-element.427), kind=kOutput, calls=%fused_computation.81 | convolution fusion | flops 16973824 | bytes 4722688 | tf_op jit(solution)/shard_map/skgt,stkd->skgd/dot_general | solution.py:97
  68.2 0.6 convolution_bitcast_fusion
  68.8 0.6 copy.98
  69.9 0.4 convert_reduce_fusion
  70.3 0.1 copy.94
  70.5 0.2 fusion.16
  70.9 18.0 %all-gather.1 = f32[64,8,4]{1,2,0:T(4,128)S(1)} all-gather(f32[4,8,4]{1,2,0:T(4,128)S(1)} %copy.87), channel_id=3, replica_groups=mesh['grp'=2,'seq'=16] {'seq'}, dimensions={0}, use_global_device_ids=true | all-gather | bytes 8704 | tf_op jit(solution)/shard_map/all_gather | solution.py:12
  88.9 19.0 %all-gather = f32[64,8,4]{1,2,0:T(4,128)S(1)} all-gather(f32[4,8,4]{1,2,0:T(4,128)S(1)} %copy.86), channel_id=2, replica_groups=mesh['grp'=2,'seq'=16] {'seq'}, dimensions={0}, use_global_device_ids=true | all-gather | bytes 8704 | tf_op jit(solution)/shard_map/all_gather | solution.py:12
  107.9 18.0 %all-gather.4 = f32[64,8,4]{1,2,0:T(4,128)S(1)} all-gather(f32[4,8,4]{1,2,0:T(4,128)S(1)} %copy.95), channel_id=6, replica_groups=mesh['grp'=2,'seq'=16] {'seq'}, dimensions={0}, use_global_device_ids=true | all-gather | bytes 8704 | tf_op jit(solution)/shard_map/all_gather | solution.py:12
  125.9 19.0 %all-gather.3 = f32[64,8,4]{1,2,0:T(4,128)S(1)} all-gather(f32[4,8,4]{1,2,0:T(4,128)S(1)} %copy.93), channel_id=5, replica_groups=mesh['grp'=2,'seq'=16] {'seq'}, dimensions={0}, use_global_device_ids=true | all-gather | bytes 8704 | tf_op jit(solution)/shard_map/all_gather | solution.py:12
  144.9 0.8 slice.30
  145.8 0.8 slice.33
  146.7 36.7 %while.25 = (s32[]{:T(128)}, f32[4,8,4]{1,2,0:T(4,128)S(1)}, f32[4,8,4]{1,2,0:T(4,128)S(1)}, f32[4,8,4,128]{3,2,1,0:T(4,128)S(1)}, f32[4,8,4]{1,2,0:T(4,128)S(1)...) while((s32[]{:T(128)}, f32[4,8,4]{1,2,0:T(4,128)S(1)}, ...), condition=%wide.region_12.13_spmd, body=%wide.region_11.12_spmd.sunk | while | flops 99845 | bytes 538823 | solution.py:17
  147.1 0.8 constant_dynamic-slice_fusion.6
  148.0 1.1 fusion.60
  149.6 0.8 constant_dynamic-slice_fusion.6
  150.4 1.1 fusion.60
  152.0 0.8 constant_dynamic-slice_fusion.6
  152.9 1.1 fusion.60
  154.5 0.8 constant_dynamic-slice_fusion.6
  155.3 1.1 fusion.60
  156.9 0.8 constant_dynamic-slice_fusion.6
  157.8 1.1 fusion.60
  159.4 0.8 constant_dynamic-slice_fusion.6
  160.2 1.1 fusion.60
  161.8 0.8 constant_dynamic-slice_fusion.6
  162.7 1.1 fusion.60
  164.3 0.8 constant_dynamic-slice_fusion.6
  165.1 1.1 fusion.60
  166.7 0.8 constant_dynamic-slice_fusion.6
  167.6 1.1 fusion.60
  169.2 0.8 constant_dynamic-slice_fusion.6
  170.0 1.1 fusion.60
  171.6 0.8 constant_dynamic-slice_fusion.6
  172.5 1.1 fusion.60
  174.1 0.8 constant_dynamic-slice_fusion.6
  174.9 1.1 fusion.60
  176.5 0.8 constant_dynamic-slice_fusion.6
  177.4 1.1 fusion.60
  179.0 0.8 constant_dynamic-slice_fusion.6
  179.8 1.1 fusion.60
  181.4 0.8 constant_dynamic-slice_fusion.6
  182.3 1.1 fusion.60
  183.6 0.1 broadcast_divide_fusion
  183.8 0.6 add_convert_fusion
  (134 shorter events, 8.4 us)
Async XLA Ops:
  6.5 138.4 %all-gather.9.cloned.1.call-start = ((), (), s32[]{:S(2)}) async-start(), calls=%async_computation | async-start | bytes 1114112 | tf_op jit(solution)/shard_map/all_gather | solution.py:12
  52.0 3.5 %copy-start = (bf16[16,128,1024]{1,2,0:T(8,128)(2,1)S(1)}, bf16[16,128,1024]{1,2,0:T(8,128)(2,1)}, u32[]{:S(2)}) copy-start(bf16[16,128,1024]{1,2,0:T(8,128)(2,1)} %copy.114) | copy-start | bytes 12582916
  52.0 6.5 %copy-start.1 = (s32[4,8,16]{2,1,0:T(8,128)S(1)}, s32[4,8,16]{2,1,0:T(8,128)}, u32[]{:S(2)}) copy-start(s32[4,8,16]{2,1,0:T(8,128)} %param.12) | copy-start | bytes 6148
  58.5 87.3 %all-gather.11.cloned.1.call-start = ((), (), s32[]{:S(2)}) async-start(), calls=%async_computation.1 | async-start | bytes 1114112 | tf_op jit(solution)/shard_map/all_gather | solution.py:12
  59.9 9.7 %copy-start.2 = (f32[4,64]{1,0:T(4,128)S(1)}, f32[4,64]{1,0:T(4,128)}, u32[]{:S(2)}) copy-start(f32[4,64]{1,0:T(4,128)} %param.9) | copy-start | bytes 3076
Sparse Core Ops, SparseCore 0:
  58.6 34.1 all-gather.8
  94.9 37.5 all-gather.10
where the time goes:
time: 193 us; the launch traced here: 191 us
  blocking collectives  97.4 us (50%)
  local copies, waits for them, and re-layouts  41.4 us (21%)
  other arithmetic  23.8 us (12%)
  matrix products  14.6 us (8%)
  between operations  13.6 us (7%)
    all_gather x4, blocking collectives, joined(): gathered = jax.tree.map(lambda a: lax.all_gather(a, axis), part)  74 us
    all_gather x1, blocking collectives, per_device(): all_queries = lax.all_gather(queries, 'seq', axis=1, tiled=True)  23.4 us
    add x15, other arithmetic, merge_pair(): left[offset + 2] * left_scale[..., None]  16.9 us
    dynamic_slice x21, local copies, waits for them, and re-layouts, take(): lax.dynamic_index_in_dim(a, source, 0, False)  14.4 us
    unnamed x11, local copies, waits for them, and re-layouts  13 us
    slice x1, local copies, waits for them, and re-layouts, per_device(): kv_pool[:, :, kv_width:].reshape(slot_count, page_len, kv_heads, HEAD_DIM)  6.11 us
    dot_general x1, matrix products, per_device(): jnp.einsum('skgt,stkd->skgd', page_wt, value_rows, preferred_element_type...  4.5 us
  transfers between devices with their start and end apart: 2, of which 0 were waited for; matrix products, arithmetic and copies ran while one was open for 7% of the time, Pallas kernels for 0%

commit v1 on v0

--- a/solution.py
+++ b/solution.py
@@ -41,7 +41,7 @@
     ctx_pages = page_table.shape[1]
     col_count = queries.shape[1]
     highest = lax.Precision.HIGHEST
-    all_queries = lax.all_gather(queries, "seq", axis=1, tiled=True)
+    all_queries = jnp.concatenate(lax.all_gather(queries, "seq"), axis=1)
     head_count = all_queries.shape[1] // HEAD_DIM
     group_size = head_count // kv_heads
     score_scale = 1.0 / math.sqrt(HEAD_DIM)

time: 193 us -> 193 us (level)
  no operation moved by 1% of the time
where the time goes in v1:
time: 193 us; the launch traced here: 191 us
  blocking collectives  97.4 us (50%)
  local copies, waits for them, and re-layouts  41.4 us (21%)
  other arithmetic  23.8 us (12%)
  matrix products  14.6 us (8%)
  between operations  13.6 us (7%)
    all_gather x4, blocking collectives, joined(): gathered = jax.tree.map(lambda a: lax.all_gather(a, axis), part)  74 us
    all_gather x1, blocking collectives, per_device(): all_queries = jnp.concatenate(lax.all_gather(queries, 'seq'), axis=1)  23.4 us
    add x15, other arithmetic, merge_pair(): left[offset + 2] * left_scale[..., None]  16.9 us
    dynamic_slice x21, local copies, waits for them, and re-layouts, take(): lax.dynamic_index_in_dim(a, source, 0, False)  14.4 us
    unnamed x11, local copies, waits for them, and re-layouts  13 us
    slice x1, local copies, waits for them, and re-layouts, per_device(): kv_pool[:, :, kv_width:].reshape(slot_count, page_len, kv_heads, HEAD_DIM)  6.11 us
    dot_general x1, matrix products, per_device(): jnp.einsum('skgt,stkd->skgd', page_wt, value_rows, preferred_element_type...  4.5 us
  transfers between devices with their start and end apart: 2, of which 0 were waited for; matrix products, arithmetic and copies ran while one was open for 7% of the time, Pallas kernels for 0%

profile of v1, /device:TPU:0, one launch (start us, length us, event | category | flops | bytes accessed | tf_op | source)
XLA Modules:
  0.0 191.3 jit_solution(13230901904686127513)
XLA Ops:
  6.5 0.9 compare_reduce_fusion.1
  7.4 0.9 fusion.21
  8.3 0.7 select_reduce_fusion.2
  9.1 0.2 convert_reduce_fusion.1
  9.3 23.4 %all-gather.7 = bf16[16,4,256]{2,1,0:T(4,128)(2,1)S(1)} all-gather(bf16[1,4,256]{2,1,0:T(4,128)(2,1)} %bitcast.111), channel_id=2, replica_groups=mesh['grp'=2,'seq'=16] {'seq'}, dimensions={0}, use_global_device_ids=true | all-gather | bytes 34816 | tf_op jit(solution)/shard_map/all_gather | solution.py:44
  32.8 0.2 convolution_convert_fusion
  33.1 6.1 %fusion.43 = (bf16[16,128,1024]{2,1,0:T(8,128)(2,1)}, bf16[16,128,1024]{2,1,0:T(8,128)(2,1)}) fusion(bf16[16,128,2048]{2,1,0:T(8,128)(2,1)} %param.10), kind=kLoop, calls=%fused_computation.82 | loop fusion | bytes 16777216 | tf_op jit(solution)/shard_map/slice | solution.py:60
  39.2 6.4 %copy.115 = bf16[16,128,1024]{1,2,0:T(8,128)(2,1)} copy(bf16[16,128,1024]{2,1,0:T(8,128)(2,1)} %get-tuple-element.421) | data formatting | bytes 8388608
  45.6 6.4 %copy.114 = bf16[16,128,1024]{1,2,0:T(8,128)(2,1)} copy(bf16[16,128,1024]{2,1,0:T(8,128)(2,1)} %get-tuple-element.422) | data formatting | bytes 8388608
  52.0 3.5 %fusion.31 = f32[16,1,8,128]{3,1,2,0:T(1,128)S(1)} fusion(bf16[16,128,8,128]{1,3,2,0:T(8,128)(2,1)} %bitcast.96, pred[16,128,1,1]{1,0,2,3:T(8,128)(4,1)S(1)} %get-tuple-element.428), kind=kOutput, calls=%fused_computation.61 | convolution fusion | flops 4194304 | bytes 4261888 | tf_op jit(solution)/shard_map/st,stkd->skd/dot_general | solution.py:71
  55.5 1.2 fusion.33
  56.8 0.3 fusion.19
  57.1 0.1 copy.108
  57.3 0.2 fusion.11
  57.6 0.9 fusion.22
  58.5 1.2 compare_reduce_fusion
  59.9 3.5 %fusion.45 = (f32[16,8,4]{2,1,0:T(8,128)S(1)}, f32[16,8,4,128]{3,2,1,0:T(4,128)S(1)}) fusion(bf16[16,8,4,128]{3,2,1,0:T(4,128)(2,1)S(1)} %reshape.113, bf16[16,128,8,128]{1,3,2,0:T(8,128)(2,1)} %bitcast.98, pred[16,128]{1,0:T(8,128)(4,1)S(1)} %get-tuple-element.427), kind=kOutput, calls=%fused_computation.84 | convolution fusion | flops 16973312 | bytes 4591616 | tf_op jit(solution)/shard_map/skgd,stkd->skgt/dot_general | solution.py:87
  63.4 0.1 copy.92
  63.6 0.1 select_reduce_fusion
  63.7 4.5 %fusion.40 = f32[16,8,4,128]{3,2,1,0:T(4,128)S(1)} fusion(bf16[16,128,8,128]{1,3,2,0:T(8,128)(2,1)} %bitcast.97, f32[16,8,4,128]{3,2,1,0:T(4,128)S(1)} %get-tuple-element.430, f32[16,8,4]{2,1,0:T(8,128)S(1)} %get-tuple-element.429, pred[16,128]{1,0:T(8,128)(4,1)S(1)} %get-tuple-element.427), kind=kOutput, calls=%fused_computation.81 | convolution fusion | flops 16973824 | bytes 4722688 | tf_op jit(solution)/shard_map/skgt,stkd->skgd/dot_general | solution.py:97
  68.2 0.6 convolution_bitcast_fusion
  68.8 0.6 copy.98
  69.9 0.4 convert_reduce_fusion
  70.3 0.1 copy.94
  70.5 0.2 fusion.16
  70.9 18.0 %all-gather.2 = f32[64,8,4]{1,2,0:T(4,128)S(1)} all-gather(f32[4,8,4]{1,2,0:T(4,128)S(1)} %copy.87), channel_id=4, replica_groups=mesh['grp'=2,'seq'=16] {'seq'}, dimensions={0}, use_global_device_ids=true | all-gather | bytes 8704 | tf_op jit(solution)/shard_map/all_gather | solution.py:12
  88.9 19.0 %all-gather.1 = f32[64,8,4]{1,2,0:T(4,128)S(1)} all-gather(f32[4,8,4]{1,2,0:T(4,128)S(1)} %copy.86), channel_id=3, replica_groups=mesh['grp'=2,'seq'=16] {'seq'}, dimensions={0}, use_global_device_ids=true | all-gather | bytes 8704 | tf_op jit(solution)/shard_map/all_gather | solution.py:12
  107.9 18.0 %all-gather.5 = f32[64,8,4]{1,2,0:T(4,128)S(1)} all-gather(f32[4,8,4]{1,2,0:T(4,128)S(1)} %copy.95), channel_id=7, replica_groups=mesh['grp'=2,'seq'=16] {'seq'}, dimensions={0}, use_global_device_ids=true | all-gather | bytes 8704 | tf_op jit(solution)/shard_map/all_gather | solution.py:12
  125.9 19.0 %all-gather.4 = f32[64,8,4]{1,2,0:T(4,128)S(1)} all-gather(f32[4,8,4]{1,2,0:T(4,128)S(1)} %copy.93), channel_id=6, replica_groups=mesh['grp'=2,'seq'=16] {'seq'}, dimensions={0}, use_global_device_ids=true | all-gather | bytes 8704 | tf_op jit(solution)/shard_map/all_gather | solution.py:12
  144.9 0.8 slice.30
  145.8 0.8 slice.33
  146.7 36.7 %while.25 = (s32[]{:T(128)}, f32[4,8,4]{1,2,0:T(4,128)S(1)}, f32[4,8,4]{1,2,0:T(4,128)S(1)}, f32[4,8,4,128]{3,2,1,0:T(4,128)S(1)}, f32[4,8,4]{1,2,0:T(4,128)S(1)...) while((s32[]{:T(128)}, f32[4,8,4]{1,2,0:T(4,128)S(1)}, ...), condition=%wide.region_12.13_spmd, body=%wide.region_11.12_spmd.sunk | while | flops 99845 | bytes 538823 | solution.py:17
  147.1 0.8 constant_dynamic-slice_fusion.6
  148.0 1.1 fusion.60
  149.6 0.8 constant_dynamic-slice_fusion.6
  150.4 1.1 fusion.60
  152.0 0.8 constant_dynamic-slice_fusion.6
  152.9 1.1 fusion.60
  154.5 0.8 constant_dynamic-slice_fusion.6
  155.3 1.1 fusion.60
  156.9 0.8 constant_dynamic-slice_fusion.6
  157.8 1.1 fusion.60
  159.4 0.8 constant_dynamic-slice_fusion.6
  160.2 1.1 fusion.60
  161.8 0.8 constant_dynamic-slice_fusion.6
  162.7 1.1 fusion.60
  164.3 0.8 constant_dynamic-slice_fusion.6
  165.1 1.1 fusion.60
  166.7 0.8 constant_dynamic-slice_fusion.6
  167.6 1.1 fusion.60
  169.2 0.8 constant_dynamic-slice_fusion.6
  170.0 1.1 fusion.60
  171.6 0.8 constant_dynamic-slice_fusion.6
  172.5 1.1 fusion.60
  174.1 0.8 constant_dynamic-slice_fusion.6
  174.9 1.1 fusion.60
  176.5 0.8 constant_dynamic-slice_fusion.6
  177.4 1.1 fusion.60
  179.0 0.8 constant_dynamic-slice_fusion.6
  179.8 1.1 fusion.60
  181.4 0.8 constant_dynamic-slice_fusion.6
  182.3 1.1 fusion.60
  183.6 0.1 broadcast_divide_fusion
  183.8 0.6 add_convert_fusion
  (134 shorter events, 8.4 us)
Async XLA Ops:
  6.5 138.4 %all-gather.11.cloned.1.call-start = ((), (), s32[]{:S(2)}) async-start(), calls=%async_computation | async-start | bytes 1114112 | tf_op jit(solution)/shard_map/all_gather | solution.py:12
  52.0 3.5 %copy-start = (bf16[16,128,1024]{1,2,0:T(8,128)(2,1)S(1)}, bf16[16,128,1024]{1,2,0:T(8,128)(2,1)}, u32[]{:S(2)}) copy-start(bf16[16,128,1024]{1,2,0:T(8,128)(2,1)} %copy.114) | copy-start | bytes 12582916
  52.0 6.5 %copy-start.1 = (s32[4,8,16]{2,1,0:T(8,128)S(1)}, s32[4,8,16]{2,1,0:T(8,128)}, u32[]{:S(2)}) copy-start(s32[4,8,16]{2,1,0:T(8,128)} %param.12) | copy-start | bytes 6148
  58.5 87.3 %all-gather.13.cloned.1.call-start = ((), (), s32[]{:S(2)}) async-start(), calls=%async_computation.1 | async-start | bytes 1114112 | tf_op jit(solution)/shard_map/all_gather | solution.py:12
  59.9 9.7 %copy-start.2 = (f32[4,64]{1,0:T(4,128)S(1)}, f32[4,64]{1,0:T(4,128)}, u32[]{:S(2)}) copy-start(f32[4,64]{1,0:T(4,128)} %param.9) | copy-start | bytes 3076
Sparse Core Ops, SparseCore 0:
  58.6 34.1 all-gather.10
  94.9 37.5 all-gather.12
